TPU v7x, 32 devices: a whole 2x2x4 slice. The times are simulated.
32 devices in a mesh: vox: 16 (over z, x, core), subj: 2 (over y).
Axes of the slice: x: 2, y: 2, z: 4, core: 2. Of those that a mesh axis runs over, the one named last changes fastest.
Arguments:
- series: bfloat16 [8, 4096, 512], P('subj', 'vox'), may hold values from -6 to 6
- live_mask: int32 [4096], P('vox'), may hold values from 0 to 1, as said below
- neighbours: int32 [4096, 13], P('vox'), may hold values from -1 to 510, as said below
- start_vectors: float32 [4096, 64], P('vox'), may hold values from -60 to 60
Outputs:
- embedding: float32 [4096, 64], P('vox')
Inputs may be any that keep to these rules, and one draw needn't show every extreme that they name: `live_mask`: within each aligned block of 128 voxel slots the live slots are a leading run of 1 to 128 slots. `neighbours`: slot n of voxel i names voxel (i // 256 - 1) * 256 + n, which is live and lies before i; the entries of a row are distinct or -1; rows of dead voxels are all -1; rows of the first 256 voxels name no slot under 256.
All inputs are finite; a program needn't handle non-finite values.
Results may differ from a plain program's by a relative error of at most 0.0024.
Values may be sent and summed in bfloat16 or wider, within the bound.
No kernel may reach another device: no remote copies, remote signals or barrier semaphores. Data moves between devices by JAX's collectives and lax.ppermute only.
A program may use at most 64 MiB of HBM per device.

v0:
```python
import math
import jax
import jax.numpy as jnp
from jax import lax
from jax.sharding import PartitionSpec as P

ITERS = 3


def shifted(shard, axis, by):
    count = lax.axis_size(axis)
    pairs = [(i, i + by) for i in range(count) if 0 <= i + by < count]
    return lax.ppermute(shard, axis, pairs)


def as_sent(shard):
    return jax.tree.map(lambda a: a.astype(jnp.bfloat16) if a.dtype == jnp.float32 else a, shard)


def standard(block):
    values = block.astype(jnp.float32)
    center = values - jnp.mean(values, axis=-1, keepdims=True)
    spread = jnp.mean(center * center, axis=-1, keepdims=True)
    return (center * lax.rsqrt(spread + 1e-05)).astype(jnp.bfloat16)


def orthonormal(images):
    gram_matrix = jnp.dot(images.T, images, precision=lax.Precision.HIGHEST)
    gram_matrix = lax.psum(gram_matrix, "vox")
    factor = jnp.linalg.cholesky(gram_matrix)
    return lax.linalg.triangular_solve(
        factor, images, left_side=False, lower=True, transpose_a=True
    )


def dense_graph(weight, slots, columns_total):
    column_ids = jnp.arange(columns_total, dtype=jnp.int32)
    matrix = jnp.zeros((weight.shape[0], columns_total), jnp.float32)
    for offset in range(weight.shape[1]):
        hits = (slots[:, offset][:, None] == column_ids[None, :]).astype(jnp.float32)
        matrix = matrix + weight[:, offset][:, None] * hits
    return matrix


def product(left, right):
    return jnp.dot(left, right, precision=lax.Precision.HIGHEST)


def on_device(series, live_mask, neighbours, start_vectors):
    voxels_here = series.shape[1]
    frames = series.shape[2]
    subjects = series.shape[0] * lax.axis_size("subj")
    scale_factor = 0.5 / math.sqrt(frames * subjects)
    zscored = standard(series)
    earlier = shifted(zscored, "vox", 1)
    window = jnp.concatenate([earlier, zscored], axis=1)
    present = neighbours >= 0
    safe_slots = jnp.maximum(neighbours, 0)
    columns = []
    for offset in range(neighbours.shape[1]):
        picked = jnp.take(window, safe_slots[:, offset], axis=1)
        columns.append(
            jnp.einsum("svf,svf->v", zscored, picked, preferred_element_type=jnp.float32)
        )
    partial_sums = jnp.stack(columns, axis=1)
    summed = lax.psum(partial_sums, "subj")
    weight = jnp.where(present, jnp.exp(scale_factor * summed), 0.0)
    living = live_mask.astype(jnp.float32)
    local_graph = dense_graph(weight, neighbours, 2 * voxels_here)
    owed = jnp.sum(local_graph, axis=0)
    received = shifted(owed[:voxels_here], "vox", -1)
    degree = 1.0 + jnp.sum(weight, axis=1) + owed[voxels_here:] + received
    scaling = living * lax.rsqrt(degree)
    vectors = living[:, None] * start_vectors
    for repeat in range(ITERS):
        scaled = scaling[:, None] * vectors
        earlier_rows = shifted(as_sent(scaled), "vox", 1).astype(scaled.dtype)
        window_rows = jnp.concatenate([earlier_rows, scaled], axis=0)
        forward = product(local_graph, window_rows)
        returns = product(local_graph.T, scaled)
        arrived = shifted(as_sent(returns[:voxels_here]), "vox", -1)
        images = 0.5 * (
            vectors + scaling[:, None] * (scaled + forward + returns[voxels_here:] + arrived)
        )
        vectors = orthonormal(images)
    return vectors


def solution(mesh):
    placed = (P("subj", "vox", None), P("vox"), P("vox", None), P("vox", None))
    return jax.shard_map(
        on_device, mesh=mesh, in_specs=placed, out_specs=P("vox", None), check_vma=False
    )
```

profile of v0, /device:TPU:0, one launch (start us, length us, event | category | flops | bytes accessed | tf_op | source)
XLA Modules:
  0.0 326.5 jit_solution(9285607745963571878)
XLA Ops:
  0.0 2.1 convert_reduce_fusion
  2.2 1.2 fusion.2
  3.4 1.6 fusion.3
  5.0 2.6 collective-permute-start
  10.2 1.4 pad_maximum_fusion
  11.6 2.5 gather_fusion.3
  14.0 2.5 gather_fusion.2
  16.5 2.5 gather_fusion.1
  19.0 2.4 gather_fusion
  21.5 2.5 gather_fusion.12
  24.0 2.5 gather_fusion.11
  26.5 2.5 gather_fusion.10
  28.9 2.4 gather_fusion.9
  31.4 2.5 gather_fusion.8
  33.9 2.5 gather_fusion.7
  36.4 2.7 gather_fusion.6
  39.1 2.5 gather_fusion.5
  41.5 2.5 gather_fusion.4
  44.1 9.5 %fusion.7 = (f32[256]{0:T(256)S(1)}, f32[256]{0:T(256)S(1)}, f32[256]{0:T(256)S(1)}, f32[256]{0:T(256)S(1)}) fusion(bf16[256,4,512]{2,1,0:T(4,128)(2,1)} %gather_fusion.3, pred[256]{0:T(512)(128)(4,1)S(1)} %get-tuple-element.72, bf16[256,4,512]{2,1,0:T(4,128)(2,1)} %gather_fusion.2, pred[256]{0:T(512)(128)(4,1)S(1)} %get-tuple-element.73, ...), kind=kLoop, calls=%fused_computation.35 | loop fusion | flops 11009024 | bytes 5256192 | tf_op jit(solution)/shard_map/svf,svf->v/dot_general | solution.py:63
  53.7 14.7 %fusion.16 = (f32[256]{0:T(256)S(1)}, f32[256]{0:T(256)S(1)}, f32[256]{0:T(256)S(1)}, f32[256]{0:T(256)S(1)}, f32[256]{0:T(256)S(1)}, /*index=5*/f32[256]{0:T(25...) fusion(bf16[256,4,512]{2,1,0:T(4,128)(2,1)S(1)} %copy-done.1, pred[256]{0:T(512)(128)(4,1)S(1)} %get-tuple-element.76, ...), kind=kLoop, calls=%fused_computation.44 | loop fusion | flops 21493504 | bytes 10505472 | tf_op jit(solution)/shard_map/svf,svf->v/dot_general | solution.py:63
  68.5 9.0 %psum.28 = f32[256,13]{0,1:T(8,128)S(1)} all-reduce(f32[256,13]{0,1:T(8,128)S(1)} %stack.55), channel_id=1, replica_groups=mesh['vox'=16,'subj'=2] {'subj'}, use_global_device_ids=true, to_apply=%region_2.0 | all-reduce | flops 3328 | bytes 26624 | tf_op jit(solution)/shard_map/psum | solution.py:66
  77.5 1.0 fusion.61
  78.5 1.3 collective-permute-start.1
  79.8 9.8 %collective-permute-done.1 = f32[256]{0:T(256)S(1)} collective-permute-done((f32[256]{0:T(256)S(1)}, f32[256]{0:T(256)S(1)}, u32[]{:S(2)}, u32[]{:S(2)}) %collective-permute-start.1) | collective-permute-done | bytes 1056 | tf_op jit(solution)/shard_map/ppermute | solution.py:13
  89.6 7.1 %collective-permute-start.2 = (bf16[256,64]{0,1:T(8,128)(2,1)S(1)}, bf16[256,64]{0,1:T(8,128)(2,1)S(1)}, u32[]{:S(2)}, u32[]{:S(2)}) collective-permute-start(bf16[256,64]{0,1:T(8,128)(2,1)S(1)} %get-tuple-element.25), channel_id=1, source_target_pairs={{0,2},{2,4},{4,6},{6,8},{8,10},{10,12},{12,14},{14,16},{16,18},{18... | collective-permute-start | bytes 98312 | tf_op jit(solution)/shard_map/ppermute | solution.py:13
  97.1 1.3 collective-permute-start.3
  98.5 1.8 collective-permute-done.3
  101.1 60.4 %psum.29 = f32[64,64]{0,1:T(8,128)S(1)} all-reduce(f32[64,64]{0,1:T(8,128)S(1)} %fusion.66), channel_id=1, replica_groups=mesh['vox'=16,'subj'=2] {'vox'}, use_global_device_ids=true, to_apply=%region_5.7 | all-reduce | flops 4096 | bytes 32768 | tf_op jit(solution)/shard_map/psum | solution.py:29
  161.6 5.8 %cholesky.59 = f32[64,64]{1,0:T(8,128)S(1)} custom-call(f32[64,64]{1,0:T(8,128)S(1)} %fusion.49), custom_call_target="Cholesky" | custom-call | tf_op jit(solution)/shard_map/jit(cholesky)/cholesky | solution.py:30
  167.5 0.6 compare_reduce_fusion.2
  168.1 0.7 fusion.41
  168.8 4.9 %custom-call.7 = f32[1,64,64]{1,2,0:T(8,128)S(1)} custom-call(f32[1,64,64]{2,1,0:T(8,128)S(1)} %fusion.41), custom_call_target="InvertDiagBlocksLowerTriangular" | custom-call | tf_op jit(solution)/shard_map/triangular_solve/custom-call.0 | solution.py:31
  174.0 1.3 collective-permute-start.4
  175.7 1.3 collective-permute-start.5
  177.1 1.8 collective-permute-done.5
  179.7 57.9 %psum.30 = f32[64,64]{0,1:T(8,128)S(1)} all-reduce(f32[64,64]{0,1:T(8,128)S(1)} %fusion.68), channel_id=1, replica_groups=mesh['vox'=16,'subj'=2] {'vox'}, use_global_device_ids=true, to_apply=%region_8.12 | all-reduce | flops 4096 | bytes 32768 | tf_op jit(solution)/shard_map/psum | solution.py:29
  237.6 5.8 %cholesky.70 = f32[64,64]{1,0:T(8,128)S(1)} custom-call(f32[64,64]{1,0:T(8,128)S(1)} %fusion.47), custom_call_target="Cholesky" | custom-call | tf_op jit(solution)/shard_map/jit(cholesky)/cholesky | solution.py:30
  243.5 0.6 compare_reduce_fusion.1
  244.2 0.7 fusion.42
  244.8 4.9 %custom-call.8 = f32[1,64,64]{1,2,0:T(8,128)S(1)} custom-call(f32[1,64,64]{2,1,0:T(8,128)S(1)} %fusion.42), custom_call_target="InvertDiagBlocksLowerTriangular" | custom-call | tf_op jit(solution)/shard_map/triangular_solve/custom-call.0 | solution.py:31
  250.0 1.3 collective-permute-start.6
  251.8 1.3 collective-permute-start.7
  253.1 1.8 collective-permute-done.7
  255.7 57.7 %psum.31 = f32[64,64]{0,1:T(8,128)S(1)} all-reduce(f32[64,64]{0,1:T(8,128)S(1)} %fusion.70), channel_id=1, replica_groups=mesh['vox'=16,'subj'=2] {'vox'}, use_global_device_ids=true, to_apply=%region_9.13 | all-reduce | flops 4096 | bytes 32768 | tf_op jit(solution)/shard_map/psum | solution.py:29
  313.6 5.8 %cholesky.81 = f32[64,64]{1,0:T(8,128)S(1)} custom-call(f32[64,64]{1,0:T(8,128)S(1)} %fusion.45), custom_call_target="Cholesky" | custom-call | tf_op jit(solution)/shard_map/jit(cholesky)/cholesky | solution.py:30
  320.1 0.7 fusion.43
  320.7 4.9 %custom-call.9 = f32[1,64,64]{1,2,0:T(8,128)S(1)} custom-call(f32[1,64,64]{2,1,0:T(8,128)S(1)} %fusion.43), custom_call_target="InvertDiagBlocksLowerTriangular" | custom-call | tf_op jit(solution)/shard_map/triangular_solve/custom-call.0 | solution.py:31
  325.6 0.9 convolution_bitcast_fusion
  (108 shorter events, 8.0 us)
Async XLA Ops:
  0.0 2.2 copy-start
  2.1 5.5 %copy-start.7 = (s32[256,13]{0,1:T(8,128)S(1)}, s32[256,13]{0,1:T(8,128)}, u32[]{:S(2)}) copy-start(s32[256,13]{0,1:T(8,128)} %param.11) | copy-start | bytes 39940
  5.0 5.2 %collective-permute-start = (bf16[4,256,512]{2,0,1:T(4,128)(2,1)S(1)}, bf16[4,256,512]{2,0,1:T(4,128)(2,1)S(1)}, u32[]{:S(2)}, u32[]{:S(2)}) collective-permute-start(bf16[4,256,512]{2,0,1:T(4,128)(2,1)S(1)} %fusion.3), channel_id=1, source_target_pairs={{0,2},{2,4},{4,6},{6,8},{8,10},{10,12},{12,14},{14,16},{16,18},{18... | collective-permute-start | bytes 3145736 | tf_op jit(solution)/shard_map/ppermute | solution.py:13
  44.0 9.6 %copy-start.1 = (bf16[256,4,512]{2,1,0:T(4,128)(2,1)S(1)}, bf16[256,4,512]{2,1,0:T(4,128)(2,1)}, u32[]{:S(2)}) copy-start(bf16[256,4,512]{2,1,0:T(4,128)(2,1)} %gather_fusion.12) | copy-start | bytes 3145732
  44.0 9.6 %copy-start.2 = (bf16[256,4,512]{2,1,0:T(4,128)(2,1)S(1)}, bf16[256,4,512]{2,1,0:T(4,128)(2,1)}, u32[]{:S(2)}) copy-start(bf16[256,4,512]{2,1,0:T(4,128)(2,1)} %gather_fusion.11) | copy-start | bytes 3145732
  44.0 9.6 %copy-start.3 = (bf16[256,4,512]{2,1,0:T(4,128)(2,1)S(1)}, bf16[256,4,512]{2,1,0:T(4,128)(2,1)}, u32[]{:S(2)}) copy-start(bf16[256,4,512]{2,1,0:T(4,128)(2,1)} %gather_fusion.10) | copy-start | bytes 3145732
  44.0 9.6 %copy-start.4 = (bf16[256,4,512]{2,1,0:T(4,128)(2,1)S(1)}, bf16[256,4,512]{2,1,0:T(4,128)(2,1)}, u32[]{:S(2)}) copy-start(bf16[256,4,512]{2,1,0:T(4,128)(2,1)} %gather_fusion.9) | copy-start | bytes 3145732
  44.0 9.6 %copy-start.5 = (bf16[256,4,512]{2,1,0:T(4,128)(2,1)S(1)}, bf16[256,4,512]{2,1,0:T(4,128)(2,1)}, u32[]{:S(2)}) copy-start(bf16[256,4,512]{2,1,0:T(4,128)(2,1)} %gather_fusion.8) | copy-start | bytes 3145732
  44.0 9.6 %copy-start.9 = (pred[256]{0:T(512)(128)(4,1)S(1)}, pred[256]{0:T(512)(128)(4,1)}, u32[]{:S(2)}) copy-start(pred[256]{0:T(512)(128)(4,1)} %get-tuple-element.78) | copy-start | bytes 772
  44.0 9.6 %copy-start.10 = (pred[256]{0:T(512)(128)(4,1)S(1)}, pred[256]{0:T(512)(128)(4,1)}, u32[]{:S(2)}) copy-start(pred[256]{0:T(512)(128)(4,1)} %get-tuple-element.79) | copy-start | bytes 772
  44.0 9.6 %copy-start.11 = (pred[256]{0:T(512)(128)(4,1)S(1)}, pred[256]{0:T(512)(128)(4,1)}, u32[]{:S(2)}) copy-start(pred[256]{0:T(512)(128)(4,1)} %get-tuple-element.80) | copy-start | bytes 772
  44.1 9.6 %copy-start.12 = (pred[256]{0:T(512)(128)(4,1)S(1)}, pred[256]{0:T(512)(128)(4,1)}, u32[]{:S(2)}) copy-start(pred[256]{0:T(512)(128)(4,1)} %get-tuple-element.81) | copy-start | bytes 772
  44.1 9.6 %copy-start.13 = (pred[256]{0:T(512)(128)(4,1)S(1)}, pred[256]{0:T(512)(128)(4,1)}, u32[]{:S(2)}) copy-start(pred[256]{0:T(512)(128)(4,1)} %get-tuple-element.82) | copy-start | bytes 772
  44.1 9.6 %copy-start.14 = (pred[256]{0:T(512)(128)(4,1)S(1)}, pred[256]{0:T(512)(128)(4,1)}, u32[]{:S(2)}) copy-start(pred[256]{0:T(512)(128)(4,1)} %get-tuple-element.83) | copy-start | bytes 772
  44.1 9.6 %copy-start.15 = (pred[256]{0:T(512)(128)(4,1)S(1)}, pred[256]{0:T(512)(128)(4,1)}, u32[]{:S(2)}) copy-start(pred[256]{0:T(512)(128)(4,1)} %compare_and_fusion.8) | copy-start | bytes 772
  53.7 26.1 %copy-start.8 = (s32[256]{0:T(256)S(1)}, s32[256]{0:T(256)}, u32[]{:S(2)}) copy-start(s32[256]{0:T(256)} %param.10) | copy-start | bytes 3076
  53.7 35.9 %copy-start.6 = (f32[256,64]{0,1:T(8,128)S(1)}, f32[256,64]{0,1:T(8,128)}, u32[]{:S(2)}) copy-start(f32[256,64]{0,1:T(8,128)} %param.12) | copy-start | bytes 196612
  78.5 11.1 %collective-permute-start.1 = (f32[256]{0:T(256)S(1)}, f32[256]{0:T(256)S(1)}, u32[]{:S(2)}, u32[]{:S(2)}) collective-permute-start(f32[256]{0:T(256)S(1)} %slice.190), channel_id=1, source_target_pairs={{2,0},{4,2},{6,4},{8,6},{10,8},{12,10},{14,12},{16,14},{18,16},{20... | collective-permute-start | bytes 3080 | tf_op jit(solution)/shard_map/ppermute | solution.py:13
  89.6 8.8 %collective-permute-start.2 = (bf16[256,64]{0,1:T(8,128)(2,1)S(1)}, bf16[256,64]{0,1:T(8,128)(2,1)S(1)}, u32[]{:S(2)}, u32[]{:S(2)}) collective-permute-start(bf16[256,64]{0,1:T(8,128)(2,1)S(1)} %get-tuple-element.25), channel_id=1, source_target_pairs={{0,2},{2,4},{4,6},{6,8},{8,10},{10,12},{12,14},{14,16},{16,18},{18... | collective-permute-start | bytes 98312 | tf_op jit(solution)/shard_map/ppermute | solution.py:13
  97.1 3.1 collective-permute-start.3
  174.0 3.1 collective-permute-start.4
  175.7 3.1 collective-permute-start.5
  250.0 3.1 collective-permute-start.6
  251.8 3.1 collective-permute-start.7
where the time goes:
time: 327 us
  blocking collectives  185 us (57%)
  other arithmetic  70 us (21%)
  local copies, waits for them, and re-layouts  32.8 us (10%)
  starting transfers between devices  17.5 us (5%)
  waiting for transfers between devices  15.1 us (5%)
  matrix products  5.26 us (2%)
    psum x3, blocking collectives, orthonormal(): gram_matrix = lax.psum(gram_matrix, 'vox')  176 us
    gather x13, local copies, waits for them, and re-layouts, on_device(): picked = jnp.take(window, safe_slots[:, offset], axis=1)  32.4 us
    dot_general x2, other arithmetic, on_device(): jnp.einsum('svf,svf->v', zscored, picked, preferred_element_type=jnp.floa...  24.1 us
    another operation x9, other arithmetic, orthonormal(): factor = jnp.linalg.cholesky(gram_matrix)  19.6 us
    ppermute x8, starting transfers between devices, shifted(): return lax.ppermute(shard, axis, pairs)  17.5 us
    another operation x6, other arithmetic, orthonormal(): lax.linalg.triangular_solve(factor, images, left_side=False, lower=True,...  16.6 us
    ppermute x8, waiting for transfers between devices, shifted(): return lax.ppermute(shard, axis, pairs)  15.1 us
    psum x1, blocking collectives, on_device(): summed = lax.psum(partial_sums, 'subj')  8.99 us
  transfers between devices with their start and end apart: 8, of which 4 were waited for; matrix products, arithmetic and copies ran while one was open for 1% of the time, Pallas kernels for 0%

commit v1 on v0

--- a/solution.py
+++ b/solution.py
@@ -26,7 +26,7 @@
 
 def orthonormal(images):
     gram_matrix = jnp.dot(images.T, images, precision=lax.Precision.HIGHEST)
-    gram_matrix = lax.psum(gram_matrix, "vox")
+    gram_matrix = lax.all_gather(gram_matrix, axis_name="vox").sum(axis=0)
     factor = jnp.linalg.cholesky(gram_matrix)
     return lax.linalg.triangular_solve(
         factor, images, left_side=False, lower=True, transpose_a=True

time: 327 us -> 219 us (0.67)
  blocking collectives: 185 us -> 74.8 us
    psum x3 -> x0, blocking collectives: 176 us -> none  [orthonormal(): gram_matrix = lax.psum(gram_matrix, 'vox')]
    all_gather x0 -> x3, blocking collectives: none -> 65.8 us  [orthonormal(): gram_matrix = lax.all_gather(gram_matrix, axis_name='vox').sum(axis=0)]
  transfers between devices with their start and end apart: 8 -> 8, of which waited for: 4 -> 4; matrix products, arithmetic and copies ran while one was open for 1% -> 2% of each run, Pallas kernels for 0% -> 0%
where the time goes in v1:
time: 219 us; the launch traced here: 218 us
  blocking collectives  74.8 us (34%)
  other arithmetic  70.2 us (32%)
  local copies, waits for them, and re-layouts  32.8 us (15%)
  starting transfers between devices  19.4 us (9%)
  waiting for transfers between devices  15.1 us (7%)
  matrix products  5.26 us (2%)
    all_gather x3, blocking collectives, orthonormal(): gram_matrix = lax.all_gather(gram_matrix, axis_name='vox').sum(axis=0)  65.8 us
    gather x13, local copies, waits for them, and re-layouts, on_device(): picked = jnp.take(window, safe_slots[:, offset], axis=1)  32.4 us
    dot_general x2, other arithmetic, on_device(): jnp.einsum('svf,svf->v', zscored, picked, preferred_element_type=jnp.floa...  24.1 us
    another operation x9, other arithmetic, orthonormal(): factor = jnp.linalg.cholesky(gram_matrix)  19.6 us
    ppermute x8, starting transfers between devices, shifted(): return lax.ppermute(shard, axis, pairs)  19.4 us
    another operation x6, other arithmetic, orthonormal(): lax.linalg.triangular_solve(factor, images, left_side=False, lower=True,...  16.6 us
    ppermute x8, waiting for transfers between devices, shifted(): return lax.ppermute(shard, axis, pairs)  15.1 us
    psum x1, blocking collectives, on_device(): summed = lax.psum(partial_sums, 'subj')  8.99 us
  transfers between devices with their start and end apart: 8, of which 4 were waited for; matrix products, arithmetic and copies ran while one was open for 2% of the time, Pallas kernels for 0%

profile of v1, /device:TPU:0, one launch (start us, length us, event | category | flops | bytes accessed | tf_op | source)
XLA Modules:
  0.0 218.3 jit_solution(9593848405151555083)
XLA Ops:
  0.0 2.1 convert_reduce_fusion
  2.2 1.2 fusion.2
  3.4 1.6 fusion.3
  5.0 2.6 %collective-permute-start = (bf16[4,256,512]{2,0,1:T(4,128)(2,1)S(1)}, bf16[4,256,512]{2,0,1:T(4,128)(2,1)S(1)}, u32[]{:S(2)}, u32[]{:S(2)}) collective-permute-start(bf16[4,256,512]{2,0,1:T(4,128)(2,1)S(1)} %fusion.3), channel_id=1, source_target_pairs={{0,2},{2,4},{4,6},{6,8},{8,10},{10,12},{12,14},{14,16},{16,18},{18... | collective-permute-start | bytes 3145736 | tf_op jit(solution)/shard_map/ppermute | solution.py:13
  10.2 1.4 pad_maximum_fusion
  11.6 2.5 %gather_fusion.3 = bf16[256,4,512]{2,1,0:T(4,128)(2,1)} fusion(bf16[4,512,512]{2,0,1:T(4,128)(2,1)S(1)} %pad_maximum_fusion, s32[1024]{0:T(1024)S(1)} %pad_clamp_fusion.9), kind=kCustom, calls=%fused_computation.3.clone | custom fusion | bytes 2098176 | tf_op jit(solution)/shard_map/jit(_take)/gather | solution.py:61
  14.0 2.5 %gather_fusion.2 = bf16[256,4,512]{2,1,0:T(4,128)(2,1)} fusion(bf16[4,512,512]{2,0,1:T(4,128)(2,1)S(1)} %pad_maximum_fusion, s32[1024]{0:T(1024)S(1)} %pad_clamp_fusion.10), kind=kCustom, calls=%fused_computation.2.clone | custom fusion | bytes 2098176 | tf_op jit(solution)/shard_map/jit(_take)/gather | solution.py:61
  16.5 2.5 %gather_fusion.1 = bf16[256,4,512]{2,1,0:T(4,128)(2,1)} fusion(bf16[4,512,512]{2,0,1:T(4,128)(2,1)S(1)} %pad_maximum_fusion, s32[1024]{0:T(1024)S(1)} %pad_clamp_fusion.11), kind=kCustom, calls=%fused_computation.1.clone | custom fusion | bytes 2098176 | tf_op jit(solution)/shard_map/jit(_take)/gather | solution.py:61
  19.0 2.4 %gather_fusion = bf16[256,4,512]{2,1,0:T(4,128)(2,1)} fusion(bf16[4,512,512]{2,0,1:T(4,128)(2,1)S(1)} %pad_maximum_fusion, s32[1024]{0:T(1024)S(1)} %pad_clamp_fusion.12), kind=kCustom, calls=%fused_computation.clone | custom fusion | bytes 2098176 | tf_op jit(solution)/shard_map/jit(_take)/gather | solution.py:61
  21.5 2.5 %gather_fusion.12 = bf16[256,4,512]{2,1,0:T(4,128)(2,1)} fusion(bf16[4,512,512]{2,0,1:T(4,128)(2,1)S(1)} %pad_maximum_fusion, s32[1024]{0:T(1024)S(1)} %pad_clamp_fusion), kind=kCustom, calls=%fused_computation.12.clone | custom fusion | bytes 2098176 | tf_op jit(solution)/shard_map/jit(_take)/gather | solution.py:61
  24.0 2.5 %gather_fusion.11 = bf16[256,4,512]{2,1,0:T(4,128)(2,1)} fusion(bf16[4,512,512]{2,0,1:T(4,128)(2,1)S(1)} %pad_maximum_fusion, s32[1024]{0:T(1024)S(1)} %pad_clamp_fusion.1), kind=kCustom, calls=%fused_computation.11.clone | custom fusion | bytes 2098176 | tf_op jit(solution)/shard_map/jit(_take)/gather | solution.py:61
  26.5 2.5 %gather_fusion.10 = bf16[256,4,512]{2,1,0:T(4,128)(2,1)} fusion(bf16[4,512,512]{2,0,1:T(4,128)(2,1)S(1)} %pad_maximum_fusion, s32[1024]{0:T(1024)S(1)} %pad_clamp_fusion.2), kind=kCustom, calls=%fused_computation.10.clone | custom fusion | bytes 2098176 | tf_op jit(solution)/shard_map/jit(_take)/gather | solution.py:61
  28.9 2.4 %gather_fusion.9 = bf16[256,4,512]{2,1,0:T(4,128)(2,1)} fusion(bf16[4,512,512]{2,0,1:T(4,128)(2,1)S(1)} %pad_maximum_fusion, s32[1024]{0:T(1024)S(1)} %pad_clamp_fusion.3), kind=kCustom, calls=%fused_computation.9.clone | custom fusion | bytes 2098176 | tf_op jit(solution)/shard_map/jit(_take)/gather | solution.py:61
  31.4 2.5 %gather_fusion.8 = bf16[256,4,512]{2,1,0:T(4,128)(2,1)} fusion(bf16[4,512,512]{2,0,1:T(4,128)(2,1)S(1)} %pad_maximum_fusion, s32[1024]{0:T(1024)S(1)} %pad_clamp_fusion.4), kind=kCustom, calls=%fused_computation.8.clone | custom fusion | bytes 2098176 | tf_op jit(solution)/shard_map/jit(_take)/gather | solution.py:61
  33.9 2.5 %gather_fusion.7 = bf16[256,4,512]{2,1,0:T(4,128)(2,1)} fusion(bf16[4,512,512]{2,0,1:T(4,128)(2,1)S(1)} %pad_maximum_fusion, s32[1024]{0:T(1024)S(1)} %pad_clamp_fusion.5), kind=kCustom, calls=%fused_computation.7.clone | custom fusion | bytes 2098176 | tf_op jit(solution)/shard_map/jit(_take)/gather | solution.py:61
  36.4 2.7 %gather_fusion.6 = bf16[256,4,512]{2,1,0:T(4,128)(2,1)} fusion(bf16[4,512,512]{2,0,1:T(4,128)(2,1)S(1)} %pad_maximum_fusion, s32[1024]{0:T(1024)S(1)} %pad_clamp_fusion.6), kind=kCustom, calls=%fused_computation.6.clone | custom fusion | bytes 2098176 | tf_op jit(solution)/shard_map/jit(_take)/gather | solution.py:61
  39.1 2.5 %gather_fusion.5 = bf16[256,4,512]{2,1,0:T(4,128)(2,1)} fusion(bf16[4,512,512]{2,0,1:T(4,128)(2,1)S(1)} %pad_maximum_fusion, s32[1024]{0:T(1024)S(1)} %pad_clamp_fusion.7), kind=kCustom, calls=%fused_computation.5.clone | custom fusion | bytes 2098176 | tf_op jit(solution)/shard_map/jit(_take)/gather | solution.py:61
  41.5 2.5 %gather_fusion.4 = bf16[256,4,512]{2,1,0:T(4,128)(2,1)} fusion(bf16[4,512,512]{2,0,1:T(4,128)(2,1)S(1)} %pad_maximum_fusion, s32[1024]{0:T(1024)S(1)} %pad_clamp_fusion.8), kind=kCustom, calls=%fused_computation.4.clone | custom fusion | bytes 2098176 | tf_op jit(solution)/shard_map/jit(_take)/gather | solution.py:61
  44.1 9.5 %fusion.7 = (f32[256]{0:T(256)S(1)}, f32[256]{0:T(256)S(1)}, f32[256]{0:T(256)S(1)}, f32[256]{0:T(256)S(1)}) fusion(bf16[256,4,512]{2,1,0:T(4,128)(2,1)} %gather_fusion.3, pred[256]{0:T(512)(128)(4,1)S(1)} %get-tuple-element.72, bf16[256,4,512]{2,1,0:T(4,128)(2,1)} %gather_fusion.2, pred[256]{0:T(512)(128)(4,1)S(1)} %get-tuple-element.73, ...), kind=kLoop, calls=%fused_computation.35 | loop fusion | flops 11009024 | bytes 5256192 | tf_op jit(solution)/shard_map/svf,svf->v/dot_general | solution.py:63
  53.7 14.7 %fusion.16 = (f32[256]{0:T(256)S(1)}, f32[256]{0:T(256)S(1)}, f32[256]{0:T(256)S(1)}, f32[256]{0:T(256)S(1)}, f32[256]{0:T(256)S(1)}, /*index=5*/f32[256]{0:T(25...) fusion(bf16[256,4,512]{2,1,0:T(4,128)(2,1)S(1)} %copy-done.1, pred[256]{0:T(512)(128)(4,1)S(1)} %get-tuple-element.76, ...), kind=kLoop, calls=%fused_computation.44 | loop fusion | flops 21493504 | bytes 10505472 | tf_op jit(solution)/shard_map/svf,svf->v/dot_general | solution.py:63
  68.5 9.0 %psum.7 = f32[256,13]{0,1:T(8,128)S(1)} all-reduce(f32[256,13]{0,1:T(8,128)S(1)} %stack.55), channel_id=1, replica_groups=mesh['vox'=16,'subj'=2] {'subj'}, use_global_device_ids=true, to_apply=%region_2.0 | all-reduce | flops 3328 | bytes 26624 | tf_op jit(solution)/shard_map/psum | solution.py:66
  77.5 1.0 fusion.61
  78.5 1.3 collective-permute-start.1
  79.8 9.8 %collective-permute-done.1 = f32[256]{0:T(256)S(1)} collective-permute-done((f32[256]{0:T(256)S(1)}, f32[256]{0:T(256)S(1)}, u32[]{:S(2)}, u32[]{:S(2)}) %collective-permute-start.1) | collective-permute-done | bytes 1056 | tf_op jit(solution)/shard_map/ppermute | solution.py:13
  89.6 7.1 %collective-permute-start.2 = (bf16[256,64]{0,1:T(8,128)(2,1)S(1)}, bf16[256,64]{0,1:T(8,128)(2,1)S(1)}, u32[]{:S(2)}, u32[]{:S(2)}) collective-permute-start(bf16[256,64]{0,1:T(8,128)(2,1)S(1)} %get-tuple-element.25), channel_id=1, source_target_pairs={{0,2},{2,4},{4,6},{6,8},{8,10},{10,12},{12,14},{14,16},{16,18},{18... | collective-permute-start | bytes 98312 | tf_op jit(solution)/shard_map/ppermute | solution.py:13
  97.1 1.3 collective-permute-start.3
  98.5 1.8 collective-permute-done.3
  101.1 23.6 %all-gather = f32[1024,64]{1,0:T(8,128)S(1)} all-gather(f32[64,64]{1,0:T(8,128)S(1)} %fusion.66), channel_id=2, replica_groups=mesh['vox'=16,'subj'=2] {'vox'}, dimensions={0}, use_global_device_ids=true | all-gather | bytes 278528 | tf_op jit(solution)/shard_map/all_gather | solution.py:29
  124.9 5.8 %cholesky.59 = f32[64,64]{1,0:T(8,128)S(1)} custom-call(f32[64,64]{1,0:T(8,128)S(1)} %fusion.49), custom_call_target="Cholesky" | custom-call | tf_op jit(solution)/shard_map/jit(cholesky)/cholesky | solution.py:30
  130.7 0.6 compare_reduce_fusion.2
  131.4 0.7 fusion.41
  132.1 4.9 %custom-call.7 = f32[1,64,64]{1,2,0:T(8,128)S(1)} custom-call(f32[1,64,64]{2,1,0:T(8,128)S(1)} %fusion.41), custom_call_target="InvertDiagBlocksLowerTriangular" | custom-call | tf_op jit(solution)/shard_map/triangular_solve/custom-call.0 | solution.py:31
  137.2 2.3 %collective-permute-start.4 = (bf16[256,64]{0,1:T(8,128)(2,1)S(1)}, bf16[256,64]{0,1:T(8,128)(2,1)S(1)}, u32[]{:S(2)}, u32[]{:S(2)}) collective-permute-start(bf16[256,64]{0,1:T(8,128)(2,1)S(1)} %get-tuple-element.23), channel_id=1, source_target_pairs={{0,2},{2,4},{4,6},{6,8},{8,10},{10,12},{12,14},{14,16},{16,18},{18... | collective-permute-start | bytes 98312 | tf_op jit(solution)/shard_map/ppermute | solution.py:13
  140.0 1.3 collective-permute-start.5
  141.3 1.8 collective-permute-done.5
  143.9 21.2 %all-gather.1 = f32[1024,64]{1,0:T(8,128)S(1)} all-gather(f32[64,64]{1,0:T(8,128)S(1)} %fusion.68), channel_id=3, replica_groups=mesh['vox'=16,'subj'=2] {'vox'}, dimensions={0}, use_global_device_ids=true | all-gather | bytes 278528 | tf_op jit(solution)/shard_map/all_gather | solution.py:29
  165.3 5.8 %cholesky.70 = f32[64,64]{1,0:T(8,128)S(1)} custom-call(f32[64,64]{1,0:T(8,128)S(1)} %fusion.47), custom_call_target="Cholesky" | custom-call | tf_op jit(solution)/shard_map/jit(cholesky)/cholesky | solution.py:30
  171.1 0.6 compare_reduce_fusion.1
  171.8 0.7 fusion.42
  172.4 4.9 %custom-call.8 = f32[1,64,64]{1,2,0:T(8,128)S(1)} custom-call(f32[1,64,64]{2,1,0:T(8,128)S(1)} %fusion.42), custom_call_target="InvertDiagBlocksLowerTriangular" | custom-call | tf_op jit(solution)/shard_map/triangular_solve/custom-call.0 | solution.py:31
  177.6 2.3 %collective-permute-start.6 = (bf16[256,64]{0,1:T(8,128)(2,1)S(1)}, bf16[256,64]{0,1:T(8,128)(2,1)S(1)}, u32[]{:S(2)}, u32[]{:S(2)}) collective-permute-start(bf16[256,64]{0,1:T(8,128)(2,1)S(1)} %get-tuple-element.21), channel_id=1, source_target_pairs={{0,2},{2,4},{4,6},{6,8},{8,10},{10,12},{12,14},{14,16},{16,18},{18... | collective-permute-start | bytes 98312 | tf_op jit(solution)/shard_map/ppermute | solution.py:13
  180.4 1.3 collective-permute-start.7
  181.7 1.8 collective-permute-done.7
  184.3 20.9 %all-gather.2 = f32[1024,64]{1,0:T(8,128)S(1)} all-gather(f32[64,64]{1,0:T(8,128)S(1)} %fusion.70), channel_id=4, replica_groups=mesh['vox'=16,'subj'=2] {'vox'}, dimensions={0}, use_global_device_ids=true | all-gather | bytes 278528 | tf_op jit(solution)/shard_map/all_gather | solution.py:29
  205.4 5.8 %cholesky.81 = f32[64,64]{1,0:T(8,128)S(1)} custom-call(f32[64,64]{1,0:T(8,128)S(1)} %fusion.45), custom_call_target="Cholesky" | custom-call | tf_op jit(solution)/shard_map/jit(cholesky)/cholesky | solution.py:30
  211.9 0.7 fusion.43
  212.5 4.9 %custom-call.9 = f32[1,64,64]{1,2,0:T(8,128)S(1)} custom-call(f32[1,64,64]{2,1,0:T(8,128)S(1)} %fusion.43), custom_call_target="InvertDiagBlocksLowerTriangular" | custom-call | tf_op jit(solution)/shard_map/triangular_solve/custom-call.0 | solution.py:31
  217.4 0.9 convolution_bitcast_fusion
  (111 shorter events, 8.1 us)
Async XLA Ops:
  0.0 2.2 copy-start
  2.1 5.5 %copy-start.7 = (s32[256,13]{0,1:T(8,128)S(1)}, s32[256,13]{0,1:T(8,128)}, u32[]{:S(2)}) copy-start(s32[256,13]{0,1:T(8,128)} %param.11) | copy-start | bytes 39940
  5.0 5.2 %collective-permute-start = (bf16[4,256,512]{2,0,1:T(4,128)(2,1)S(1)}, bf16[4,256,512]{2,0,1:T(4,128)(2,1)S(1)}, u32[]{:S(2)}, u32[]{:S(2)}) collective-permute-start(bf16[4,256,512]{2,0,1:T(4,128)(2,1)S(1)} %fusion.3), channel_id=1, source_target_pairs={{0,2},{2,4},{4,6},{6,8},{8,10},{10,12},{12,14},{14,16},{16,18},{18... | collective-permute-start | bytes 3145736 | tf_op jit(solution)/shard_map/ppermute | solution.py:13
  44.0 9.6 %copy-start.1 = (bf16[256,4,512]{2,1,0:T(4,128)(2,1)S(1)}, bf16[256,4,512]{2,1,0:T(4,128)(2,1)}, u32[]{:S(2)}) copy-start(bf16[256,4,512]{2,1,0:T(4,128)(2,1)} %gather_fusion.12) | copy-start | bytes 3145732
  44.0 9.6 %copy-start.2 = (bf16[256,4,512]{2,1,0:T(4,128)(2,1)S(1)}, bf16[256,4,512]{2,1,0:T(4,128)(2,1)}, u32[]{:S(2)}) copy-start(bf16[256,4,512]{2,1,0:T(4,128)(2,1)} %gather_fusion.11) | copy-start | bytes 3145732
  44.0 9.6 %copy-start.3 = (bf16[256,4,512]{2,1,0:T(4,128)(2,1)S(1)}, bf16[256,4,512]{2,1,0:T(4,128)(2,1)}, u32[]{:S(2)}) copy-start(bf16[256,4,512]{2,1,0:T(4,128)(2,1)} %gather_fusion.10) | copy-start | bytes 3145732
  44.0 9.6 %copy-start.4 = (bf16[256,4,512]{2,1,0:T(4,128)(2,1)S(1)}, bf16[256,4,512]{2,1,0:T(4,128)(2,1)}, u32[]{:S(2)}) copy-start(bf16[256,4,512]{2,1,0:T(4,128)(2,1)} %gather_fusion.9) | copy-start | bytes 3145732
  44.0 9.6 %copy-start.5 = (bf16[256,4,512]{2,1,0:T(4,128)(2,1)S(1)}, bf16[256,4,512]{2,1,0:T(4,128)(2,1)}, u32[]{:S(2)}) copy-start(bf16[256,4,512]{2,1,0:T(4,128)(2,1)} %gather_fusion.8) | copy-start | bytes 3145732
  44.0 9.6 %copy-start.9 = (pred[256]{0:T(512)(128)(4,1)S(1)}, pred[256]{0:T(512)(128)(4,1)}, u32[]{:S(2)}) copy-start(pred[256]{0:T(512)(128)(4,1)} %get-tuple-element.78) | copy-start | bytes 772
  44.0 9.6 %copy-start.10 = (pred[256]{0:T(512)(128)(4,1)S(1)}, pred[256]{0:T(512)(128)(4,1)}, u32[]{:S(2)}) copy-start(pred[256]{0:T(512)(128)(4,1)} %get-tuple-element.79) | copy-start | bytes 772
  44.0 9.6 %copy-start.11 = (pred[256]{0:T(512)(128)(4,1)S(1)}, pred[256]{0:T(512)(128)(4,1)}, u32[]{:S(2)}) copy-start(pred[256]{0:T(512)(128)(4,1)} %get-tuple-element.80) | copy-start | bytes 772
  44.1 9.6 %copy-start.12 = (pred[256]{0:T(512)(128)(4,1)S(1)}, pred[256]{0:T(512)(128)(4,1)}, u32[]{:S(2)}) copy-start(pred[256]{0:T(512)(128)(4,1)} %get-tuple-element.81) | copy-start | bytes 772
  44.1 9.6 %copy-start.13 = (pred[256]{0:T(512)(128)(4,1)S(1)}, pred[256]{0:T(512)(128)(4,1)}, u32[]{:S(2)}) copy-start(pred[256]{0:T(512)(128)(4,1)} %get-tuple-element.82) | copy-start | bytes 772
  44.1 9.6 %copy-start.14 = (pred[256]{0:T(512)(128)(4,1)S(1)}, pred[256]{0:T(512)(128)(4,1)}, u32[]{:S(2)}) copy-start(pred[256]{0:T(512)(128)(4,1)} %get-tuple-element.83) | copy-start | bytes 772
  44.1 9.6 %copy-start.15 = (pred[256]{0:T(512)(128)(4,1)S(1)}, pred[256]{0:T(512)(128)(4,1)}, u32[]{:S(2)}) copy-start(pred[256]{0:T(512)(128)(4,1)} %compare_and_fusion.8) | copy-start | bytes 772
  53.7 26.1 %copy-start.8 = (s32[256]{0:T(256)S(1)}, s32[256]{0:T(256)}, u32[]{:S(2)}) copy-start(s32[256]{0:T(256)} %param.10) | copy-start | bytes 3076
  53.7 35.9 %copy-start.6 = (f32[256,64]{0,1:T(8,128)S(1)}, f32[256,64]{0,1:T(8,128)}, u32[]{:S(2)}) copy-start(f32[256,64]{0,1:T(8,128)} %param.12) | copy-start | bytes 196612
  78.5 11.1 %collective-permute-start.1 = (f32[256]{0:T(256)S(1)}, f32[256]{0:T(256)S(1)}, u32[]{:S(2)}, u32[]{:S(2)}) collective-permute-start(f32[256]{0:T(256)S(1)} %slice.190), channel_id=1, source_target_pairs={{2,0},{4,2},{6,4},{8,6},{10,8},{12,10},{14,12},{16,14},{18,16},{20... | collective-permute-start | bytes 3080 | tf_op jit(solution)/shard_map/ppermute | solution.py:13
  89.6 8.8 %collective-permute-start.2 = (bf16[256,64]{0,1:T(8,128)(2,1)S(1)}, bf16[256,64]{0,1:T(8,128)(2,1)S(1)}, u32[]{:S(2)}, u32[]{:S(2)}) collective-permute-start(bf16[256,64]{0,1:T(8,128)(2,1)S(1)} %get-tuple-element.25), channel_id=1, source_target_pairs={{0,2},{2,4},{4,6},{6,8},{8,10},{10,12},{12,14},{14,16},{16,18},{18... | collective-permute-start | bytes 98312 | tf_op jit(solution)/shard_map/ppermute | solution.py:13
  97.1 3.1 %collective-permute-start.3 = (bf16[256,64]{0,1:T(8,128)(2,1)S(1)}, bf16[256,64]{0,1:T(8,128)(2,1)S(1)}, u32[]{:S(2)}, u32[]{:S(2)}) collective-permute-start(bf16[256,64]{0,1:T(8,128)(2,1)S(1)} %slice.264), channel_id=1, source_target_pairs={{2,0},{4,2},{6,4},{8,6},{10,8},{12,10},{14,12},{16,14},{18,16},{20... | collective-permute-start | bytes 98312 | tf_op jit(solution)/shard_map/ppermute | solution.py:13
  137.2 4.0 %collective-permute-start.4 = (bf16[256,64]{0,1:T(8,128)(2,1)S(1)}, bf16[256,64]{0,1:T(8,128)(2,1)S(1)}, u32[]{:S(2)}, u32[]{:S(2)}) collective-permute-start(bf16[256,64]{0,1:T(8,128)(2,1)S(1)} %get-tuple-element.23), channel_id=1, source_target_pairs={{0,2},{2,4},{4,6},{6,8},{8,10},{10,12},{12,14},{14,16},{16,18},{18... | collective-permute-start | bytes 98312 | tf_op jit(solution)/shard_map/ppermute | solution.py:13
  140.0 3.1 %collective-permute-start.5 = (bf16[256,64]{0,1:T(8,128)(2,1)S(1)}, bf16[256,64]{0,1:T(8,128)(2,1)S(1)}, u32[]{:S(2)}, u32[]{:S(2)}) collective-permute-start(bf16[256,64]{0,1:T(8,128)(2,1)S(1)} %slice.263), channel_id=1, source_target_pairs={{2,0},{4,2},{6,4},{8,6},{10,8},{12,10},{14,12},{16,14},{18,16},{20... | collective-permute-start | bytes 98312 | tf_op jit(solution)/shard_map/ppermute | solution.py:13
  177.6 4.0 %collective-permute-start.6 = (bf16[256,64]{0,1:T(8,128)(2,1)S(1)}, bf16[256,64]{0,1:T(8,128)(2,1)S(1)}, u32[]{:S(2)}, u32[]{:S(2)}) collective-permute-start(bf16[256,64]{0,1:T(8,128)(2,1)S(1)} %get-tuple-element.21), channel_id=1, source_target_pairs={{0,2},{2,4},{4,6},{6,8},{8,10},{10,12},{12,14},{14,16},{16,18},{18... | collective-permute-start | bytes 98312 | tf_op jit(solution)/shard_map/ppermute | solution.py:13
  180.4 3.1 %collective-permute-start.7 = (bf16[256,64]{0,1:T(8,128)(2,1)S(1)}, bf16[256,64]{0,1:T(8,128)(2,1)S(1)}, u32[]{:S(2)}, u32[]{:S(2)}) collective-permute-start(bf16[256,64]{0,1:T(8,128)(2,1)S(1)} %slice.262), channel_id=1, source_target_pairs={{2,0},{4,2},{6,4},{8,6},{10,8},{12,10},{14,12},{16,14},{18,16},{20... | collective-permute-start | bytes 98312 | tf_op jit(solution)/shard_map/ppermute | solution.py:13
